TPU v7x, 128 devices: a whole 4x4x4 slice. The times are simulated.
128 devices in a mesh: tiles: 32 (over x, y, core), reps: 4 (over z).
Axes of the slice: x: 4, y: 4, z: 4, core: 2. Of those that a mesh axis runs over, the one named last changes fastest.
Arguments:
- tiles_w: bfloat16 [4096, 128, 128], P('tiles'), may hold values from 0.0001 to 4
- tile_worker: int32 [4096], P('tiles'), may hold values from 0 to 15
- tile_owner: int32 [4096], P('tiles'), may hold values from 0 to 31
- owner_block: int32 [32, 32], P('tiles'), may hold values from 0 to 1
- worker_base: float32 [65536], P('tiles'), may hold values from -6 to 6
- worker_noise: float32 [65536], P('tiles'), may hold values from 0.2 to 1.5
- worker_cluster: int32 [65536], P('tiles'), may hold values from 0 to 255
- firm_base: float32 [8192], P('tiles'), may hold values from -6 to 6
- firm_noise: float32 [8192], P('tiles'), may hold values from 0.2 to 1.5
- firm_cluster: int32 [8192], P('tiles'), may hold values from 0 to 255
- signs: int32 [256, 256], P('reps'), may hold values from 0 to 1
- covariates: float32 [8192, 512], P('tiles'), may hold values from -0.0625 to 0.0625
- whitening: float32 [512, 512], replicated, may hold values from -0.25 to 0.25
Outputs:
- worker_effect: float32 [256, 65536], P('reps', 'tiles')
- firm_effect: float32 [256, 8192], P('reps', 'tiles')
- coefficients: float32 [256, 512], P('reps')
- covariance: float32 [512, 512], P('tiles')
Inputs may be any that keep to these rules, and one draw needn't show every extreme that they name: `tile_worker`: local worker block of each tile. `tile_owner`: owner of each tile's firm block. `owner_block`: firm block among the owner's 2 blocks. `signs`: a bit that gives the sign 2 b - 1.
All inputs are finite; a program needn't handle non-finite values.
Results may differ from a plain program's by a relative error of at most 0.0023.
Values may be sent and summed in bfloat16 or wider, within the bound.
No kernel may reach another device: no remote copies, remote signals or barrier semaphores. Data moves between devices by JAX's collectives and lax.ppermute only.
A program may use at most 64 MiB of HBM per device.

v0:
```python
import jax
import jax.numpy as jnp
from jax import lax
from jax.sharding import PartitionSpec as P

WORK_BLOCKS = 16
FIRM_BLOCKS = 2
SWEEPS = 6
spectral_bound = 0.8


def chebyshev_weights(sweep_count):
    weights = [1.0]
    weights.append(1.0 / (1.0 - 0.5 * spectral_bound * spectral_bound))
    while len(weights) < sweep_count:
        weights.append(1.0 / (1.0 - 0.25 * spectral_bound * spectral_bound * weights[-1]))
    return weights


def one_hot_rows(indices, row_count):
    return (indices[None, :] == jnp.arange(row_count, dtype=jnp.int32)[:, None]).astype(jnp.float32)


def wild_outcome(base_value, noise_scale, cluster, flip_table):
    clusters_hot = (
        cluster[None, :] == jnp.arange(flip_table.shape[1], dtype=jnp.int32)[:, None]
    ).astype(jnp.bfloat16)
    flip_values = jnp.dot(flip_table, clusters_hot, preferred_element_type=jnp.float32)
    return base_value[None, :] + noise_scale[None, :] * flip_values


def body(
    tiles_w,
    tile_worker,
    tile_owner,
    owner_block,
    worker_base,
    worker_noise,
    worker_cluster,
    firm_base,
    firm_noise,
    firm_cluster,
    signs,
    covariates,
    whitening,
):
    highest = lax.Precision.HIGHEST
    owners_count = lax.axis_size("tiles")
    tile_cells = tiles_w.shape[1]
    replicas_here = signs.shape[0]
    flip_table = (2 * signs - 1).astype(jnp.bfloat16)
    worker_outcome = wild_outcome(worker_base, worker_noise, worker_cluster, flip_table).reshape(
        replicas_here, WORK_BLOCKS, tile_cells
    )
    firm_outcome = wild_outcome(firm_base, firm_noise, firm_cluster, flip_table).reshape(
        replicas_here, FIRM_BLOCKS, tile_cells
    )
    row_mass = jnp.sum(tiles_w, axis=2, dtype=jnp.float32)
    col_mass = jnp.sum(tiles_w, axis=1, dtype=jnp.float32)
    worker_hot = one_hot_rows(tile_worker, WORK_BLOCKS)
    worker_scale = 1.0 + jnp.einsum("bt,tw->bw", worker_hot, row_mass, precision=highest)
    owner_hot = one_hot_rows(tile_owner, owners_count)
    my_blocks = owner_block[0]
    tile_block = tile_owner * FIRM_BLOCKS + jnp.sum(
        jnp.where(owner_hot > 0, my_blocks[:, None], 0), axis=0
    )
    dense_hot = one_hot_rows(tile_block, owners_count * FIRM_BLOCKS)
    firm_mass = lax.psum_scatter(
        jnp.einsum("nt,tf->nf", dense_hot, col_mass, precision=highest),
        "tiles",
        scatter_dimension=0,
        tiled=True,
    )
    firm_scale = 1.0 + firm_mass
    omegas = chebyshev_weights(SWEEPS)
    firm_older = jnp.zeros((replicas_here, FIRM_BLOCKS, tile_cells), jnp.float32)
    firm_newer = firm_older
    firm_now = firm_older
    worker_now = worker_outcome
    tile_firm = None
    for sweep_index in range(SWEEPS):
        if sweep_index == 0:
            worker_now = worker_outcome
        else:
            pulled = jnp.einsum(
                "twf,rtf->rtw", tiles_w, tile_firm, preferred_element_type=jnp.float32
            )
            worker_sum = jnp.einsum("bt,rtw->rbw", worker_hot, pulled, precision=highest)
            worker_now = worker_outcome - worker_sum / worker_scale[None]
        worker_round = worker_now.astype(jnp.bfloat16)
        tile_values = jnp.take(worker_round, tile_worker, axis=1)
        pushed = jnp.einsum(
            "twf,rtw->rtf", tiles_w, tile_values, preferred_element_type=jnp.float32
        )
        firm_sum = lax.psum_scatter(
            jnp.einsum("nt,rtf->rnf", dense_hot, pushed, precision=highest),
            "tiles",
            scatter_dimension=1,
            tiled=True,
        )
        firm_target = firm_outcome - firm_sum / firm_scale[None]
        firm_now = firm_older + omegas[sweep_index] * (firm_target - firm_older)
        firm_older, firm_newer = (firm_newer, firm_now)
        if sweep_index + 1 < SWEEPS:
            firm_round = firm_now.astype(jnp.bfloat16)
            every_firm = lax.all_gather(firm_round, "tiles", axis=1, tiled=True)
            tile_firm = jnp.take(every_firm, tile_block, axis=1)
    worker_effect = worker_now.reshape(replicas_here, WORK_BLOCKS * tile_cells)
    firm_flat = firm_now.reshape(replicas_here, FIRM_BLOCKS * tile_cells)
    mixing = jnp.dot(covariates, whitening.T, precision=highest)
    local_term = jnp.dot(firm_flat, mixing, precision=highest)
    summed = lax.psum(local_term, "tiles")
    share_rows = summed.shape[1] // owners_count
    own_columns = lax.dynamic_slice_in_dim(
        summed, lax.axis_index("tiles") * share_rows, share_rows, 1
    )
    moment = jnp.dot(own_columns.T, summed, precision=highest)
    covariance = lax.psum(moment, "reps") / (replicas_here * lax.axis_size("reps"))
    return (worker_effect, firm_flat, summed, covariance)


def solution(mesh):
    placed = (
        P("tiles", None, None),
        P("tiles"),
        P("tiles"),
        P("tiles", None),
        P("tiles"),
        P("tiles"),
        P("tiles"),
        P("tiles"),
        P("tiles"),
        P("tiles"),
        P("reps", None),
        P("tiles", None),
        P(),
    )
    return jax.shard_map(
        body,
        mesh=mesh,
        in_specs=placed,
        out_specs=(P("reps", "tiles"), P("reps", "tiles"), P("reps", None), P("tiles", None)),
        check_vma=False,
    )
```

profile of v0, /device:TPU:6, one launch (start us, length us, event | category | flops | bytes accessed | tf_op | source)
XLA Modules:
  0.0 1033.3 jit_solution(7390925900868006559)
XLA Ops:
  16.6 4.2 fusion.56
  28.9 109.8 %all-reduce = f32[64,128]{1,0:T(8,128)S(1)} all-reduce(f32[64,128]{1,0:T(8,128)S(1)} %fusion.164), channel_id=3, replica_groups=mesh['tiles'=32,'reps'=4] {'tiles'}, use_global_device_ids=true, to_apply=%region_3.0.clone | all-reduce | flops 8192 | bytes 65536
  140.8 57.8 %all-gather.6.cloned.1.call-done = bf16[64,64,128]{2,0,1:T(8,128)(2,1)} async-done(((bf16[64,2,128]{2,0,1:T(8,128)(2,1)}), bf16[64,64,128]{2,0,1:T(8,128)(2,1)}) %all-gather.6.cloned.1.call-update) | async-done | bytes 1048592 | tf_op jit(solution)/shard_map/all_gather | solution.py:106
  202.0 5.8 convolution_bitcast_fusion.9
  217.9 4.2 fusion.59
  225.1 78.4 %reduce-scatter.9.cloned.1.call-done = f32[64,2,128]{2,0,1:T(8,128)} async-done(((f32[64,64,128]{2,0,1:T(8,128)}), f32[64,2,128]{2,0,1:T(8,128)}) %reduce-scatter.9.cloned.1.call-update) | async-done | bytes 65552 | tf_op jit(solution)/shard_map/reduce_scatter | solution.py:95
  305.0 43.0 %all-gather.8.cloned.1.call-done = bf16[64,64,128]{2,0,1:T(8,128)(2,1)} async-done(((bf16[64,2,128]{2,0,1:T(8,128)(2,1)}), bf16[64,64,128]{2,0,1:T(8,128)(2,1)}) %all-gather.8.cloned.1.call-update) | async-done | bytes 1048592 | tf_op jit(solution)/shard_map/all_gather | solution.py:106
  351.3 5.8 convolution_bitcast_fusion.7
  367.3 4.2 fusion.62
  374.2 78.4 %reduce-scatter.11.cloned.1.call-done = f32[64,2,128]{2,0,1:T(8,128)} async-done(((f32[64,64,128]{2,0,1:T(8,128)}), f32[64,2,128]{2,0,1:T(8,128)}) %reduce-scatter.11.cloned.1.call-update) | async-done | bytes 65552 | tf_op jit(solution)/shard_map/reduce_scatter | solution.py:95
  454.2 43.0 %all-gather.10.cloned.1.call-done = bf16[64,64,128]{2,0,1:T(8,128)(2,1)} async-done(((bf16[64,2,128]{2,0,1:T(8,128)(2,1)}), bf16[64,64,128]{2,0,1:T(8,128)(2,1)}) %all-gather.10.cloned.1.call-update) | async-done | bytes 1048592 | tf_op jit(solution)/shard_map/all_gather | solution.py:106
  500.5 5.7 convolution_bitcast_fusion.5
  516.4 4.2 fusion.65
  523.6 78.4 %reduce-scatter.13.cloned.1.call-done = f32[64,2,128]{2,0,1:T(8,128)} async-done(((f32[64,64,128]{2,0,1:T(8,128)}), f32[64,2,128]{2,0,1:T(8,128)}) %reduce-scatter.13.cloned.1.call-update) | async-done | bytes 65552 | tf_op jit(solution)/shard_map/reduce_scatter | solution.py:95
  603.5 43.1 %all-gather.12.cloned.1.call-done = bf16[64,64,128]{2,0,1:T(8,128)(2,1)} async-done(((bf16[64,2,128]{2,0,1:T(8,128)(2,1)}), bf16[64,64,128]{2,0,1:T(8,128)(2,1)}) %all-gather.12.cloned.1.call-update) | async-done | bytes 1048592 | tf_op jit(solution)/shard_map/all_gather | solution.py:106
  650.0 5.8 convolution_bitcast_fusion.3
  665.9 4.2 fusion.68
  672.9 78.4 %reduce-scatter.15.cloned.1.call-done = f32[64,2,128]{2,0,1:T(8,128)} async-done(((f32[64,64,128]{2,0,1:T(8,128)}), f32[64,2,128]{2,0,1:T(8,128)}) %reduce-scatter.15.cloned.1.call-update) | async-done | bytes 65552 | tf_op jit(solution)/shard_map/reduce_scatter | solution.py:95
  752.8 43.0 %all-gather.14.cloned.1.call-done = bf16[64,64,128]{2,0,1:T(8,128)(2,1)} async-done(((bf16[64,2,128]{2,0,1:T(8,128)(2,1)}), bf16[64,64,128]{2,0,1:T(8,128)(2,1)}) %all-gather.14.cloned.1.call-update) | async-done | bytes 1048592 | tf_op jit(solution)/shard_map/all_gather | solution.py:106
  799.1 5.8 convolution_bitcast_fusion.1
  815.1 4.2 fusion.71
  824.1 76.3 %reduce-scatter.17.cloned.1.call-done = f32[64,2,128]{2,0,1:T(8,128)} async-done(((f32[64,64,128]{2,0,1:T(8,128)}), f32[64,2,128]{2,0,1:T(8,128)}) %reduce-scatter.17.cloned.1.call-update) | async-done | bytes 65552 | tf_op jit(solution)/shard_map/reduce_scatter | solution.py:95
  903.4 102.1 %all-reduce.3.cloned.1.call-done = f32[64,512]{1,0:T(8,128)} async-done(((f32[64,512]{1,0:T(8,128)}), f32[64,512]{1,0:T(8,128)}) %all-reduce.3.cloned.1.call-update) | async-done | bytes 131088 | tf_op jit(solution)/shard_map/psum | solution.py:112
  1006.8 17.3 %psum.15 = f32[16,512]{1,0:T(8,128)S(1)} all-reduce(f32[16,512]{1,0:T(8,128)S(1)} %fusion.162), channel_id=1, replica_groups=mesh['tiles'=32,'reps'=4] {'reps'}, use_global_device_ids=true, to_apply=%region_11.14 | all-reduce | flops 8192 | bytes 65536 | tf_op jit(solution)/shard_map/psum | solution.py:118
  (113 shorter events, 115.5 us)
Async XLA Ops:
  7.2 814.9 %copy-start = (f32[512,512]{1,0:T(8,128)S(1)}, f32[512,512]{1,0:T(8,128)}, u32[]{:S(2)}) copy-start(f32[512,512]{1,0:T(8,128)} %param.29) | copy-start | bytes 3145732
  7.2 3.1 copy-start.11
  7.2 3.1 copy-start.6
  7.2 131.7 %reduce-scatter.7.cloned.1.call-start = ((), (), s32[]{:S(2)}) async-start(), calls=%async_computation.6 | async-start | bytes 2162688 | tf_op jit(solution)/shard_map/reduce_scatter | solution.py:95
  23.4 175.2 %all-gather.6.cloned.1.call-start = ((), (), s32[]{:S(2)}) async-start(), calls=%async_computation.7 | async-start | bytes 1081344 | tf_op jit(solution)/shard_map/all_gather | solution.py:106
  25.2 113.4 %copy-start.7 = (s32[64,256]{1,0:T(8,128)S(1)}, s32[64,256]{1,0:T(8,128)}, u32[]{:S(2)}) copy-start(s32[64,256]{1,0:T(8,128)} %param.27) | copy-start | bytes 196612
  25.2 113.4 %copy-start.8 = (s32[256]{0:T(256)S(1)}, s32[256]{0:T(256)}, u32[]{:S(2)}) copy-start(s32[256]{0:T(256)} %param.26) | copy-start | bytes 3076
  25.2 113.4 %copy-start.9 = (f32[256]{0:T(256)S(1)}, f32[256]{0:T(256)}, u32[]{:S(2)}) copy-start(f32[256]{0:T(256)} %param.25) | copy-start | bytes 3076
  25.3 113.4 %copy-start.10 = (f32[256]{0:T(256)S(1)}, f32[256]{0:T(256)}, u32[]{:S(2)}) copy-start(f32[256]{0:T(256)} %param.24) | copy-start | bytes 3076
  25.3 115.4 %copy-start.5 = (s32[128]{0:T(128)S(1)}, s32[128]{0:T(128)}, u32[]{:S(2)}) copy-start(s32[128]{0:T(128)} %param.18) | copy-start | bytes 1540
  140.4 163.1 %reduce-scatter.9.cloned.1.call-start = ((), (), s32[]{:S(2)}) async-start(), calls=%async_computation.8 | async-start | bytes 2162688 | tf_op jit(solution)/shard_map/reduce_scatter | solution.py:95
  225.0 122.9 %all-gather.8.cloned.1.call-start = ((), (), s32[]{:S(2)}) async-start(), calls=%async_computation.9 | async-start | bytes 1081344 | tf_op jit(solution)/shard_map/all_gather | solution.py:106
  305.0 147.6 %reduce-scatter.11.cloned.1.call-start = ((), (), s32[]{:S(2)}) async-start(), calls=%async_computation.10 | async-start | bytes 2162688 | tf_op jit(solution)/shard_map/reduce_scatter | solution.py:95
  374.2 78.4 %copy-start.2 = (f32[64,2,128]{2,0,1:T(8,128)S(1)}, f32[64,2,128]{2,0,1:T(8,128)}, u32[]{:S(2)}) copy-start(f32[64,2,128]{2,0,1:T(8,128)} %reduce-scatter.7.cloned.1.call-done) | copy-start | bytes 196612
  374.2 122.9 %all-gather.10.cloned.1.call-start = ((), (), s32[]{:S(2)}) async-start(), calls=%async_computation.11 | async-start | bytes 1081344 | tf_op jit(solution)/shard_map/all_gather | solution.py:106
  454.1 147.9 %reduce-scatter.13.cloned.1.call-start = ((), (), s32[]{:S(2)}) async-start(), calls=%async_computation.12 | async-start | bytes 2162688 | tf_op jit(solution)/shard_map/reduce_scatter | solution.py:95
  523.5 78.4 %copy-start.3 = (f32[64,2,128]{2,0,1:T(8,128)S(1)}, f32[64,2,128]{2,0,1:T(8,128)}, u32[]{:S(2)}) copy-start(f32[64,2,128]{2,0,1:T(8,128)} %reduce-scatter.9.cloned.1.call-done) | copy-start | bytes 196612
  523.6 123.1 %all-gather.12.cloned.1.call-start = ((), (), s32[]{:S(2)}) async-start(), calls=%async_computation.13 | async-start | bytes 1081344 | tf_op jit(solution)/shard_map/all_gather | solution.py:106
  603.5 147.8 %reduce-scatter.15.cloned.1.call-start = ((), (), s32[]{:S(2)}) async-start(), calls=%async_computation.14 | async-start | bytes 2162688 | tf_op jit(solution)/shard_map/reduce_scatter | solution.py:95
  672.9 122.9 %all-gather.14.cloned.1.call-start = ((), (), s32[]{:S(2)}) async-start(), calls=%async_computation.15 | async-start | bytes 1081344 | tf_op jit(solution)/shard_map/all_gather | solution.py:106
  752.8 147.7 %reduce-scatter.17.cloned.1.call-start = ((), (), s32[]{:S(2)}) async-start(), calls=%async_computation.16 | async-start | bytes 2162688 | tf_op jit(solution)/shard_map/reduce_scatter | solution.py:95
  822.0 1.0 copy-start.1
  822.0 183.5 %all-reduce.3.cloned.1.call-start = ((), (), s32[]{:S(2)}) async-start(), calls=%async_computation.17 | async-start | bytes 262144 | tf_op jit(solution)/shard_map/psum | solution.py:112
  901.3 124.9 %copy-start.4 = (f32[64,256]{1,0:T(8,128)}, f32[64,256]{1,0:T(8,128)S(1)}, u32[]{:S(2)}) copy-start(f32[64,256]{1,0:T(8,128)S(1)} %copy_bitcast_fusion.1) | copy-start | bytes 196612
  (1 other events, 0.7 us)
Sparse Core Ops, SparseCore 0:
  23.5 80.7 reduce-scatter.6
  140.5 58.0 all-gather.5
  225.2 78.2 reduce-scatter.8
  306.1 41.7 all-gather.7
  374.3 78.2 reduce-scatter.10
  455.3 41.7 all-gather.9
  523.7 78.2 reduce-scatter.12
  604.8 41.7 all-gather.11
  673.0 78.2 reduce-scatter.14
  753.9 41.7 all-gather.13
  822.2 78.2 reduce-scatter.16
  904.1 101.3 all-reduce.2
where the time goes:
time: 1040 us; the launch traced here: 1030 us
  waiting for transfers between devices  722 us (69%)
  blocking collectives  127 us (12%)
  matrix products  103 us (10%)
  local copies, waits for them, and re-layouts  51.7 us (5%)
  between operations  15.5 us (1%)
  other arithmetic  13.9 us (1%)
    reduce_scatter x6, waiting for transfers between devices, body(): lax.psum_scatter(jnp.einsum('nt,rtf->rnf', dense_hot, pushed, precision=h...  390 us
    all_gather x5, waiting for transfers between devices, body(): every_firm = lax.all_gather(firm_round, 'tiles', axis=1, tiled=True)  230 us
    unnamed x1, blocking collectives  110 us
    psum x1, waiting for transfers between devices, body(): summed = lax.psum(local_term, 'tiles')  102 us
    dot_general x5, matrix products, body(): jnp.einsum('twf,rtf->rtw', tiles_w, tile_firm, preferred_element_type=jnp...  28.7 us
    dot_general x6, matrix products, body(): jnp.einsum('nt,rtf->rnf', dense_hot, pushed, precision=highest)  24.9 us
    dot_general x6, matrix products, body(): jnp.einsum('twf,rtw->rtf', tiles_w, tile_values, preferred_element_type=j...  24.6 us
  transfers between devices with their start and end apart: 12, of which 11 were waited for; matrix products, arithmetic and copies ran while one was open for 1% of the time, Pallas kernels for 0%

commit v1 on v0

--- a/solution.py
+++ b/solution.py
@@ -1,12 +1,21 @@
+import functools
 import jax
 import jax.numpy as jnp
 from jax import lax
 from jax.sharding import PartitionSpec as P
+from jax.lax import all_gather
 
 WORK_BLOCKS = 16
 FIRM_BLOCKS = 2
 SWEEPS = 6
 spectral_bound = 0.8
+
+
+def signs_divide(original, shard_axis):
+    return jnp.sum(all_gather(original, axis_name=shard_axis), 0)
+
+
+_hold_indices = functools.partial(signs_divide, shard_axis="tiles")
 
 
 def chebyshev_weights(sweep_count):
@@ -109,7 +118,7 @@
     firm_flat = firm_now.reshape(replicas_here, FIRM_BLOCKS * tile_cells)
     mixing = jnp.dot(covariates, whitening.T, precision=highest)
     local_term = jnp.dot(firm_flat, mixing, precision=highest)
-    summed = lax.psum(local_term, "tiles")
+    summed = _hold_indices(local_term)
     share_rows = summed.shape[1] // owners_count
     own_columns = lax.dynamic_slice_in_dim(
         summed, lax.axis_index("tiles") * share_rows, share_rows, 1

time: 1040 us -> 985 us (0.947)
  waiting for transfers between devices: 722 us -> 665 us
    psum x1 -> x0, waiting for transfers between devices: 102 us -> none  [body(): summed = lax.psum(local_term, 'tiles')]
    all_gather x0 -> x1, waiting for transfers between devices: none -> 45.1 us  [signs_divide(): return jnp.sum(all_gather(original, axis_name=shard_axis), 0)]
where the time goes in v1:
time: 985 us; the launch traced here: 976 us
  waiting for transfers between devices  665 us (68%)
  blocking collectives  127 us (13%)
  matrix products  102 us (10%)
  local copies, waits for them, and re-layouts  50.2 us (5%)
  other arithmetic  16.4 us (2%)
  between operations  15.5 us (2%)
    reduce_scatter x6, waiting for transfers between devices, body(): lax.psum_scatter(jnp.einsum('nt,rtf->rnf', dense_hot, pushed, precision=h...  390 us
    all_gather x5, waiting for transfers between devices, body(): every_firm = lax.all_gather(firm_round, 'tiles', axis=1, tiled=True)  230 us
    unnamed x1, blocking collectives  110 us
    all_gather x1, waiting for transfers between devices, signs_divide(): return jnp.sum(all_gather(original, axis_name=shard_axis), 0)  45.1 us
    dot_general x5, matrix products, body(): jnp.einsum('twf,rtf->rtw', tiles_w, tile_firm, preferred_element_type=jnp...  28.8 us
    dot_general x6, matrix products, body(): jnp.einsum('nt,rtf->rnf', dense_hot, pushed, precision=highest)  24.9 us
    dot_general x6, matrix products, body(): jnp.einsum('twf,rtw->rtf', tiles_w, tile_values, preferred_element_type=j...  24.6 us
  transfers between devices with their start and end apart: 12, of which 11 were waited for; matrix products, arithmetic and copies ran while one was open for 1% of the time, Pallas kernels for 0%

profile of v1, /device:TPU:6, one launch (start us, length us, event | category | flops | bytes accessed | tf_op | source)
XLA Modules:
  0.0 976.3 jit_solution(13301707793977460149)
XLA Ops:
  16.6 4.2 fusion.56
  28.9 109.7 %all-reduce = f32[64,128]{1,0:T(8,128)S(1)} all-reduce(f32[64,128]{1,0:T(8,128)S(1)} %fusion.164), channel_id=4, replica_groups=mesh['tiles'=32,'reps'=4] {'tiles'}, use_global_device_ids=true, to_apply=%region_3.0.clone | all-reduce | flops 8192 | bytes 65536
  140.8 57.8 %all-gather.8.cloned.1.call-done = bf16[64,64,128]{2,0,1:T(8,128)(2,1)} async-done(((bf16[64,2,128]{2,0,1:T(8,128)(2,1)}), bf16[64,64,128]{2,0,1:T(8,128)(2,1)}) %all-gather.8.cloned.1.call-update) | async-done | bytes 1048592 | tf_op jit(solution)/shard_map/all_gather | solution.py:115
  202.0 5.8 convolution_bitcast_fusion.9
  217.9 4.2 fusion.59
  225.1 78.4 %reduce-scatter.9.cloned.1.call-done = f32[64,2,128]{2,0,1:T(8,128)} async-done(((f32[64,64,128]{2,0,1:T(8,128)}), f32[64,2,128]{2,0,1:T(8,128)}) %reduce-scatter.9.cloned.1.call-update) | async-done | bytes 65552 | tf_op jit(solution)/shard_map/reduce_scatter | solution.py:104
  305.0 43.0 %all-gather.10.cloned.1.call-done = bf16[64,64,128]{2,0,1:T(8,128)(2,1)} async-done(((bf16[64,2,128]{2,0,1:T(8,128)(2,1)}), bf16[64,64,128]{2,0,1:T(8,128)(2,1)}) %all-gather.10.cloned.1.call-update) | async-done | bytes 1048592 | tf_op jit(solution)/shard_map/all_gather | solution.py:115
  351.4 5.8 convolution_bitcast_fusion.7
  367.3 4.2 fusion.62
  374.3 78.4 %reduce-scatter.11.cloned.1.call-done = f32[64,2,128]{2,0,1:T(8,128)} async-done(((f32[64,64,128]{2,0,1:T(8,128)}), f32[64,2,128]{2,0,1:T(8,128)}) %reduce-scatter.11.cloned.1.call-update) | async-done | bytes 65552 | tf_op jit(solution)/shard_map/reduce_scatter | solution.py:104
  454.2 43.0 %all-gather.12.cloned.1.call-done = bf16[64,64,128]{2,0,1:T(8,128)(2,1)} async-done(((bf16[64,2,128]{2,0,1:T(8,128)(2,1)}), bf16[64,64,128]{2,0,1:T(8,128)(2,1)}) %all-gather.12.cloned.1.call-update) | async-done | bytes 1048592 | tf_op jit(solution)/shard_map/all_gather | solution.py:115
  500.6 5.8 convolution_bitcast_fusion.5
  516.5 4.2 fusion.65
  523.7 78.4 %reduce-scatter.13.cloned.1.call-done = f32[64,2,128]{2,0,1:T(8,128)} async-done(((f32[64,64,128]{2,0,1:T(8,128)}), f32[64,2,128]{2,0,1:T(8,128)}) %reduce-scatter.13.cloned.1.call-update) | async-done | bytes 65552 | tf_op jit(solution)/shard_map/reduce_scatter | solution.py:104
  603.6 43.1 %all-gather.14.cloned.1.call-done = bf16[64,64,128]{2,0,1:T(8,128)(2,1)} async-done(((bf16[64,2,128]{2,0,1:T(8,128)(2,1)}), bf16[64,64,128]{2,0,1:T(8,128)(2,1)}) %all-gather.14.cloned.1.call-update) | async-done | bytes 1048592 | tf_op jit(solution)/shard_map/all_gather | solution.py:115
  650.1 5.8 convolution_bitcast_fusion.3
  666.0 4.2 fusion.68
  673.0 78.4 %reduce-scatter.15.cloned.1.call-done = f32[64,2,128]{2,0,1:T(8,128)} async-done(((f32[64,64,128]{2,0,1:T(8,128)}), f32[64,2,128]{2,0,1:T(8,128)}) %reduce-scatter.15.cloned.1.call-update) | async-done | bytes 65552 | tf_op jit(solution)/shard_map/reduce_scatter | solution.py:104
  752.9 43.0 %all-gather.16.cloned.1.call-done = bf16[64,64,128]{2,0,1:T(8,128)(2,1)} async-done(((bf16[64,2,128]{2,0,1:T(8,128)(2,1)}), bf16[64,64,128]{2,0,1:T(8,128)(2,1)}) %all-gather.16.cloned.1.call-update) | async-done | bytes 1048592 | tf_op jit(solution)/shard_map/all_gather | solution.py:115
  799.2 5.8 convolution_bitcast_fusion.1
  815.2 4.2 fusion.71
  824.2 76.3 %reduce-scatter.17.cloned.1.call-done = f32[64,2,128]{2,0,1:T(8,128)} async-done(((f32[64,64,128]{2,0,1:T(8,128)}), f32[64,2,128]{2,0,1:T(8,128)}) %reduce-scatter.17.cloned.1.call-update) | async-done | bytes 65552 | tf_op jit(solution)/shard_map/reduce_scatter | solution.py:104
  903.5 45.1 %all-gather.18.cloned.1.call-done = f32[2048,512]{1,0:T(8,128)} async-done(((f32[64,512]{1,0:T(8,128)}), f32[2048,512]{1,0:T(8,128)}) %all-gather.18.cloned.1.call-update) | async-done | bytes 4194320 | tf_op jit(solution)/shard_map/all_gather | solution.py:15
  951.4 17.3 %psum.7 = f32[16,512]{1,0:T(8,128)S(1)} all-reduce(f32[16,512]{1,0:T(8,128)S(1)} %fusion.162), channel_id=1, replica_groups=mesh['tiles'=32,'reps'=4] {'reps'}, use_global_device_ids=true, to_apply=%region_11.14 | all-reduce | flops 8192 | bytes 65536 | tf_op jit(solution)/shard_map/psum | solution.py:127
  (115 shorter events, 115.5 us)
Async XLA Ops:
  7.2 815.0 %copy-start = (f32[512,512]{1,0:T(8,128)S(1)}, f32[512,512]{1,0:T(8,128)}, u32[]{:S(2)}) copy-start(f32[512,512]{1,0:T(8,128)} %param.29) | copy-start | bytes 3145732
  7.2 3.1 copy-start.12
  7.2 3.1 copy-start.7
  7.2 131.7 %reduce-scatter.7.cloned.1.call-start = ((), (), s32[]{:S(2)}) async-start(), calls=%async_computation.6 | async-start | bytes 2162688 | tf_op jit(solution)/shard_map/reduce_scatter | solution.py:104
  23.4 175.3 %all-gather.8.cloned.1.call-start = ((), (), s32[]{:S(2)}) async-start(), calls=%async_computation.7 | async-start | bytes 1081344 | tf_op jit(solution)/shard_map/all_gather | solution.py:115
  25.2 113.4 %copy-start.8 = (s32[64,256]{1,0:T(8,128)S(1)}, s32[64,256]{1,0:T(8,128)}, u32[]{:S(2)}) copy-start(s32[64,256]{1,0:T(8,128)} %param.27) | copy-start | bytes 196612
  25.2 113.4 %copy-start.9 = (s32[256]{0:T(256)S(1)}, s32[256]{0:T(256)}, u32[]{:S(2)}) copy-start(s32[256]{0:T(256)} %param.26) | copy-start | bytes 3076
  25.3 113.4 %copy-start.10 = (f32[256]{0:T(256)S(1)}, f32[256]{0:T(256)}, u32[]{:S(2)}) copy-start(f32[256]{0:T(256)} %param.25) | copy-start | bytes 3076
  25.3 113.4 %copy-start.11 = (f32[256]{0:T(256)S(1)}, f32[256]{0:T(256)}, u32[]{:S(2)}) copy-start(f32[256]{0:T(256)} %param.24) | copy-start | bytes 3076
  25.3 115.4 %copy-start.6 = (s32[128]{0:T(128)S(1)}, s32[128]{0:T(128)}, u32[]{:S(2)}) copy-start(s32[128]{0:T(128)} %param.18) | copy-start | bytes 1540
  140.4 163.1 %reduce-scatter.9.cloned.1.call-start = ((), (), s32[]{:S(2)}) async-start(), calls=%async_computation.8 | async-start | bytes 2162688 | tf_op jit(solution)/shard_map/reduce_scatter | solution.py:104
  225.1 122.9 %all-gather.10.cloned.1.call-start = ((), (), s32[]{:S(2)}) async-start(), calls=%async_computation.9 | async-start | bytes 1081344 | tf_op jit(solution)/shard_map/all_gather | solution.py:115
  305.0 147.7 %reduce-scatter.11.cloned.1.call-start = ((), (), s32[]{:S(2)}) async-start(), calls=%async_computation.10 | async-start | bytes 2162688 | tf_op jit(solution)/shard_map/reduce_scatter | solution.py:104
  374.2 78.4 %copy-start.3 = (f32[64,2,128]{2,0,1:T(8,128)S(1)}, f32[64,2,128]{2,0,1:T(8,128)}, u32[]{:S(2)}) copy-start(f32[64,2,128]{2,0,1:T(8,128)} %reduce-scatter.7.cloned.1.call-done) | copy-start | bytes 196612
  374.3 122.9 %all-gather.12.cloned.1.call-start = ((), (), s32[]{:S(2)}) async-start(), calls=%async_computation.11 | async-start | bytes 1081344 | tf_op jit(solution)/shard_map/all_gather | solution.py:115
  454.2 147.9 %reduce-scatter.13.cloned.1.call-start = ((), (), s32[]{:S(2)}) async-start(), calls=%async_computation.12 | async-start | bytes 2162688 | tf_op jit(solution)/shard_map/reduce_scatter | solution.py:104
  523.6 78.4 %copy-start.4 = (f32[64,2,128]{2,0,1:T(8,128)S(1)}, f32[64,2,128]{2,0,1:T(8,128)}, u32[]{:S(2)}) copy-start(f32[64,2,128]{2,0,1:T(8,128)} %reduce-scatter.9.cloned.1.call-done) | copy-start | bytes 196612
  523.6 123.1 %all-gather.14.cloned.1.call-start = ((), (), s32[]{:S(2)}) async-start(), calls=%async_computation.13 | async-start | bytes 1081344 | tf_op jit(solution)/shard_map/all_gather | solution.py:115
  603.6 147.8 %reduce-scatter.15.cloned.1.call-start = ((), (), s32[]{:S(2)}) async-start(), calls=%async_computation.14 | async-start | bytes 2162688 | tf_op jit(solution)/shard_map/reduce_scatter | solution.py:104
  672.9 122.9 %all-gather.16.cloned.1.call-start = ((), (), s32[]{:S(2)}) async-start(), calls=%async_computation.15 | async-start | bytes 1081344 | tf_op jit(solution)/shard_map/all_gather | solution.py:115
  752.8 147.7 %reduce-scatter.17.cloned.1.call-start = ((), (), s32[]{:S(2)}) async-start(), calls=%async_computation.16 | async-start | bytes 2162688 | tf_op jit(solution)/shard_map/reduce_scatter | solution.py:104
  822.1 126.4 %all-gather.18.cloned.1.call-start = ((), (), s32[]{:S(2)}) async-start(), calls=%async_computation.17 | async-start | bytes 4325376 | tf_op jit(solution)/shard_map/all_gather | solution.py:15
  901.4 49.7 %copy-start.5 = (f32[64,256]{1,0:T(8,128)}, f32[64,256]{1,0:T(8,128)S(1)}, u32[]{:S(2)}) copy-start(f32[64,256]{1,0:T(8,128)S(1)} %copy_bitcast_fusion.1) | copy-start | bytes 196612
  951.1 18.2 %copy-start.1 = (f32[64,512]{1,0:T(8,128)}, f32[64,512]{1,0:T(8,128)S(1)}, u32[]{:S(2)}) copy-start(f32[64,512]{1,0:T(8,128)S(1)} %reduce_sum.39) | copy-start | bytes 393220
  (2 other events, 1.7 us)
Sparse Core Ops, SparseCore 0:
  23.5 80.8 reduce-scatter.6
  140.5 58.0 all-gather.7
  225.2 78.2 reduce-scatter.8
  306.2 41.7 all-gather.9
  374.4 78.2 reduce-scatter.10
  455.4 41.7 all-gather.11
  523.8 78.2 reduce-scatter.12
  604.9 41.7 all-gather.13
  673.0 78.2 reduce-scatter.14
  754.0 41.7 all-gather.15
  822.2 78.2 reduce-scatter.16
  903.2 45.2 all-gather.17
